TPU v7x, 256 devices: a whole 4x4x8 slice. The times are simulated.
256 devices in a mesh: img: 16 (over x, z_lo, core), patch: 16 (over y, z_hi).
Axes of the slice: x: 4, y: 4, z: 8 (z_hi: 4, z_lo: 2; z = z_hi * 2 + z_lo), core: 2. Of those that a mesh axis runs over, the one named last changes fastest.
Arguments:
- hidden: bfloat16 [32, 16, 128, 640], P('img', 'patch'), may hold values from -100 to 100
- stale_attn_in: bfloat16 [32, 16, 128, 640], P('img', 'patch'), may hold values from -100 to 100
- stale_conv_in: bfloat16 [32, 16, 128, 640], P('img', 'patch'), may hold values from -6 to 6
- ln_gain: float32 [640], replicated, may hold values from 0.25 to 1.75
- ln_bias: float32 [640], replicated, may hold values from -2 to 2
- w_qkv: bfloat16 [640, 1920], replicated, may hold values from -3 to 3
- w_out: bfloat16 [640, 640], replicated, may hold values from -0.25 to 0.25
- gn_gain: float32 [640], replicated, may hold values from 0.25 to 1.75
- gn_bias: float32 [640], replicated, may hold values from -1.5 to 1.5
- conv_weight: bfloat16 [3, 3, 640, 640], replicated, may hold values from -0.078125 to 0.078125
- conv_bias: float32 [640], replicated, may hold values from -1.5 to 1.5
- time_shift: float32 [32, 640], P('img'), may hold values from -6 to 6
Outputs:
- block_out: bfloat16 [32, 16, 128, 640], P('img', 'patch')
All inputs are finite; a program needn't handle non-finite values.
Results may differ from a plain program's by a relative error of at most 0.0075.
The roundings to bfloat16 on the way count: a program that leaves them out, or rounds other values in their place, can miss the bound.
Values may be sent and summed in bfloat16 or wider, within the bound.
No kernel may reach another device: no remote copies, remote signals or barrier semaphores. Data moves between devices by JAX's collectives and lax.ppermute only.
A program may use at most 128 MiB of HBM per device.

v0:
```python
import functools
import jax
import jax.numpy as jnp
from jax import lax
from jax.sharding import Mesh
from jax.sharding import PartitionSpec as P

GROUPS = 32
HEAD_DIM = 64
PATCH = ("patch_0", "patch_1")
EPSILON = 1e-05


def over_axes(shard, axes):
    return functools.reduce(lax.psum, axes, shard)


def extended(block, sides, width):
    for axis, dim in sides:
        count = lax.axis_size(axis)
        forward = [(i, i + 1) for i in range(count - 1)]
        backward = [(target, source) for source, target in forward]
        low = lax.ppermute(
            lax.slice_in_dim(block, block.shape[dim] - width, None, axis=dim), axis, forward
        )
        high = lax.ppermute(lax.slice_in_dim(block, 0, width, axis=dim), axis, backward)
        block = jnp.concatenate([low, block, high], axis=dim)
    return block


def layer_norm(values, gain, bias):
    values = values.astype(jnp.float32)
    centre = jnp.mean(values, -1, keepdims=True)
    centred = values - centre
    spread = jnp.mean(centred * centred, -1, keepdims=True)
    return (centred * lax.rsqrt(spread + EPSILON) * gain + bias).astype(jnp.bfloat16)


def absorb(softmax_state, queries, key_rows, value_rows, blocked):
    running_max, weight_sum, accum = softmax_state
    samples, key_count, channels = key_rows.shape
    head_count = channels // HEAD_DIM
    keys_split = key_rows.reshape(samples, key_count, head_count, HEAD_DIM)
    values_split = value_rows.reshape(samples, key_count, head_count, HEAD_DIM)
    scores = jnp.einsum(
        "sqhd,skhd->shqk", queries, keys_split, preferred_element_type=jnp.float32
    ) * HEAD_DIM ** (-0.5)
    scores = jnp.where(blocked[None, None, None, :], -jnp.inf, scores)
    new_max = jnp.maximum(running_max, jnp.max(scores, -1))
    rescale = jnp.exp(running_max - new_max)
    weights = jnp.exp(scores - new_max[..., None])
    weight_sum = weight_sum * rescale + jnp.sum(weights, -1)
    accum = accum * rescale[..., None] + jnp.einsum(
        "shqk,skhd->shqd",
        weights.astype(jnp.bfloat16),
        values_split,
        preferred_element_type=jnp.float32,
    )
    return (new_max, weight_sum, accum)


def shards(
    hidden,
    stale_attn_in,
    stale_conv_in,
    ln_gain,
    ln_bias,
    w_qkv,
    w_out,
    gn_gain,
    gn_bias,
    conv_weight,
    conv_bias,
    time_shift,
):
    samples, rows_dev, col_count, channels = hidden.shape
    head_count = channels // HEAD_DIM
    local_count = rows_dev * col_count
    own_start = lax.axis_index(PATCH) * local_count
    fresh_in = layer_norm(hidden, ln_gain, ln_bias).reshape(samples, local_count, channels)
    stale_in = layer_norm(stale_attn_in, ln_gain, ln_bias).reshape(samples, local_count, channels)
    fresh_qkv = jnp.einsum(
        "stc,cd->std", fresh_in, w_qkv, preferred_element_type=jnp.float32
    ).astype(jnp.bfloat16)
    queries = fresh_qkv[..., :channels].reshape(samples, local_count, head_count, HEAD_DIM)
    w_pair = w_qkv[:, channels:]
    initial = (
        jnp.full((samples, head_count, local_count), -jnp.inf, jnp.float32),
        jnp.zeros((samples, head_count, local_count), jnp.float32),
        jnp.zeros((samples, head_count, local_count, HEAD_DIM), jnp.float32),
    )
    no_block = jnp.zeros((local_count,), bool)
    softmax_state = absorb(
        initial,
        queries,
        fresh_qkv[..., channels : 2 * channels],
        fresh_qkv[..., 2 * channels :],
        no_block,
    )
    block_rows = lax.all_gather(stale_in, PATCH, axis=1, tiled=True)
    pair_rows = jnp.einsum(
        "snc,cd->snd", block_rows, w_pair, preferred_element_type=jnp.float32
    ).astype(jnp.bfloat16)
    positions = jnp.arange(block_rows.shape[1], dtype=jnp.int32)
    blocked = (positions >= own_start) & (positions < own_start + local_count)
    softmax_state = absorb(
        softmax_state, queries, pair_rows[..., :channels], pair_rows[..., channels:], blocked
    )
    running_max, weight_sum, accum = softmax_state
    attended = (
        (accum / weight_sum[..., None])
        .transpose(0, 2, 1, 3)
        .reshape(samples, local_count, channels)
        .astype(jnp.bfloat16)
    )
    attention_out = jnp.einsum("stc,cd->std", attended, w_out, preferred_element_type=jnp.float32)
    residual = (
        hidden.reshape(samples, local_count, channels).astype(jnp.float32) + attention_out
    ).astype(jnp.bfloat16)
    grouped = residual.astype(jnp.float32).reshape(samples, local_count, GROUPS, channels // GROUPS)
    cell_count = lax.axis_size(PATCH) * local_count * (channels // GROUPS)
    group_total, group_squares = (
        over_axes(jnp.sum(grouped, axis=(1, 3)), PATCH),
        over_axes(jnp.sum(grouped * grouped, axis=(1, 3)), PATCH),
    )
    group_mean = group_total / cell_count
    group_var = group_squares / cell_count - group_mean * group_mean
    centred = grouped - group_mean[:, None, :, None]
    normalized = (centred * lax.rsqrt(group_var + EPSILON)[:, None, :, None]).reshape(
        samples, local_count, channels
    )
    activated = (
        jax.nn.silu(normalized * gn_gain + gn_bias)
        .astype(jnp.bfloat16)
        .reshape(samples, rows_dev, col_count, channels)
    )
    stale_framed = extended(stale_conv_in, ((PATCH, 1),), 1)
    framed = jnp.concatenate([stale_framed[:, :1], activated, stale_framed[:, rows_dev + 1 :]], 1)
    framed = jnp.pad(framed, ((0, 0), (0, 0), (1, 1), (0, 0)))
    windows = [
        framed[:, tap_row : tap_row + rows_dev, tap_col : tap_col + col_count, :]
        for tap_row in range(3)
        for tap_col in range(3)
    ]
    unfolded = jnp.concatenate(windows, -1).reshape(samples * local_count, 9 * channels)
    convolved = jnp.dot(
        unfolded, conv_weight.reshape(9 * channels, channels), preferred_element_type=jnp.float32
    )
    summed_out = (
        convolved.reshape(samples, rows_dev, col_count, channels)
        + conv_bias
        + time_shift[:, None, None, :]
        + residual.astype(jnp.float32).reshape(samples, rows_dev, col_count, channels)
    )
    return summed_out.astype(jnp.bfloat16)


def solution(mesh):
    split = Mesh(mesh.devices.reshape(mesh.shape["img"], 4, 4), ("img", "patch_0", "patch_1"))
    return jax.shard_map(
        shards,
        mesh=split,
        in_specs=(
            P("img", PATCH, None, None),
            P("img", PATCH, None, None),
            P("img", PATCH, None, None),
            P(),
            P(),
            P(),
            P(),
            P(),
            P(),
            P(),
            P(),
            P("img", None),
        ),
        out_specs=P("img", PATCH, None, None),
        check_vma=False,
    )
```

profile of v0, /device:TPU:2, one launch (start us, length us, event | category | flops | bytes accessed | tf_op | source)
XLA Modules:
  0.0 191.6 jit_solution(10955897671697256372)
XLA Ops:
  6.5 1.2 convert_reduce_fusion.1
  7.7 1.2 fusion.54
  8.9 1.9 %fusion.57 = bf16[2,1,128,640]{3,2,0,1:T(8,128)(2,1)} fusion(bf16[2,1,128,640]{3,2,1,0:T(8,128)(2,1)} %param.13, f32[2,128]{1,0:T(2,128)S(1)} %add_rsqrt_fusion.1, f32[2,128]{1,0:T(2,128)S(1)} %broadcast_multiply_fusion.1, f32[640]{0:T(1024)} %param.16, f32[640]{0:T(1024)} %param.15), kind=kLoop, calls=%fused_computation.59 | loop fusion | flops 983040 | bytes 662528 | tf_op jit(solution)/shard_map/convert_element_type | solution.py:36
  10.9 0.0 all-gather.3.cloned.1.call-update
  10.9 1.3 collective-permute-start.1
  12.2 5.8 %collective-permute-start = (bf16[2,1,128,640]{3,2,0,1:T(8,128)(2,1)}, bf16[2,1,128,640]{3,2,0,1:T(8,128)(2,1)S(1)}, u32[]{:S(2)}, u32[]{:S(2)}) collective-permute-start(bf16[2,1,128,640]{3,2,0,1:T(8,128)(2,1)} %bitcast.118), channel_id=1, source_target_pairs={{0,1},{1,2},{2,3},{3,4},{4,5},{5,6},{6,7},{7,8},{8,9},{9,10},{10,1... | collective-permute-start | bytes 983048 | tf_op jit(solution)/shard_map/ppermute | solution.py:23
  18.0 1.1 convert_reduce_fusion
  19.1 1.2 fusion.50
  20.3 2.9 %convolution_convert_fusion.1 = bf16[2,128,1920]{2,1,0:T(8,128)(2,1)S(1)} fusion(bf16[640,1920]{1,0:T(8,128)(2,1)} %param.17, bf16[2,1,128,640]{3,2,1,0:T(8,128)(2,1)} %param.12, f32[640]{0:T(1024)} %param.16, f32[640]{0:T(1024)} %param.15, f32[2,128]{1,0:T(2,128)S(1)} %add_rsqrt_fusion.2, f32[2,128]{1,0:T(2,128)S(1)} %broadcast_multiply_fusion.2), kind=kOutput, calls=%fused_computation.13 | convolution fusion | flops 630620160 | bytes 3775488 | tf_op jit(solution)/shard_map/stc,cd->std/dot_general | solution.py:82
  23.3 0.1 fusion.78
  23.4 0.2 copy.27
  23.6 0.2 copy.28
  23.8 0.9 copy.29
  24.7 0.4 fusion.79
  25.1 0.2 fusion.41
  25.3 75.6 %all-gather.3.cloned.1.call-done = bf16[2,1,2048,640]{3,2,0,1:T(8,128)(2,1)} async-done(((bf16[2,1,128,640]{3,2,0,1:T(8,128)(2,1)}), bf16[2,1,2048,640]{3,2,0,1:T(8,128)(2,1)}) %all-gather.3.cloned.1.call-update) | async-done | bytes 5242896 | tf_op jit(solution)/shard_map/all_gather | solution.py:100
  101.0 13.2 %convolution_convert_fusion = bf16[2,2048,1280]{1,2,0:T(8,128)(2,1)} fusion(bf16[2,1,2048,640]{3,2,0,1:T(8,128)(2,1)} %all-gather.3.cloned.1.call-done, bf16[640,1920]{1,0:T(8,128)(2,1)} %param.17), kind=kOutput, calls=%fused_computation.5 | convolution fusion | flops 6716129280 | bytes 17367040 | tf_op jit(solution)/shard_map/snc,cd->snd/dot_general | solution.py:101
  114.2 10.2 %fusion.77 = (bf16[2,2048,640]{1,2,0:T(8,128)(2,1)}, bf16[2,2048,640]{1,2,0:T(8,128)(2,1)}) fusion(bf16[2,2048,1280]{1,2,0:T(8,128)(2,1)} %convolution_convert_fusion), kind=kLoop, calls=%fused_computation.99 | loop fusion | bytes 20971520 | tf_op jit(solution)/shard_map/slice | solution.py:107
  124.4 5.1 %fusion = (f32[2,10,128]{2,1,0:T(8,128)S(1)}, f32[2,10,128,2048]{3,2,1,0:T(8,128)S(1)}) fusion(pred[2048]{0:T(1024)(128)(4,1)S(1)} %fusion.72, bf16[2,128,10,64]{1,3,2,0:T(8,128)(2,1)S(1)} %bitcast.112, bf16[2,2048,10,64]{1,3,2,0:T(8,128)(2,1)} %bitcast.109), kind=kOutput, calls=%fused_computation.2 | convolution fusion | flops 686814720 | bytes 26554368 | tf_op jit(solution)/shard_map/sqhd,skhd->shqk/dot_general | solution.py:45
  129.5 4.7 %fusion.1 = f32[2,10,128]{2,1,0:T(8,128)S(1)} fusion(f32[2,10,128,2048]{3,2,1,0:T(8,128)S(1)} %get-tuple-element.24, f32[2,10,128]{2,1,0:T(8,128)S(1)} %max.18, pred[2048]{0:T(1024)(128)(4,1)S(1)} %fusion.72), kind=kLoop, calls=%fused_computation.3 | loop fusion | flops 20968960 | bytes 20994048 | tf_op jit(solution)/shard_map/reduce_sum | solution.py:52
  134.2 2.3 %copy-done.1 = f32[2,10,128,2048]{3,2,1,0:T(8,128)} copy-done((f32[2,10,128,2048]{3,2,1,0:T(8,128)}, f32[2,10,128,2048]{3,2,1,0:T(8,128)S(1)}, u32[]{:S(2)}) %copy-start.1) | copy-done | bytes 20971544
  136.5 10.8 %fusion.17 = f32[2,128,10,64]{1,3,2,0:T(8,128)S(1)} fusion(bf16[2,2048,10,64]{1,3,2,0:T(8,128)(2,1)} %bitcast.110, f32[2,10,128,2048]{3,2,1,0:T(8,128)} %copy-done.1, f32[2,10,128]{2,1,0:T(8,128)S(1)} %max.18, pred[2048]{0:T(1024)(128)(4,1)S(1)} %fusion.72), kind=kOutput, calls=%fused_computation.26 | convolution fusion | flops 692060160 | bytes 26882048 | tf_op jit(solution)/shard_map/shqk,skhd->shqd/dot_general | solution.py:53
  147.3 0.0 copy-start.2
  147.4 0.0 copy-start.4
  147.4 0.0 copy-start.5
  147.4 0.3 fusion.31
  147.8 0.5 copy-done.2
  148.3 0.5 fusion.75
  148.8 0.1 reduce_sum.102
  148.9 0.1 reduce_sum.99
  149.1 0.1 reduce_sum.103
  149.1 0.1 reduce_sum.100
  149.2 10.2 %all-reduce.2 = (f32[2,32]{1,0:T(2,128)S(1)}, f32[2,32]{1,0:T(2,128)S(1)}) all-reduce(f32[2,32]{1,0:T(2,128)S(1)} %reduce_sum.103, f32[2,32]{1,0:T(2,128)S(1)} %reduce_sum.100), channel_id=1, replica_groups=mesh['img'=16,'patch_0'=4,'patch_1'=4] {'patch_0'}, use_global_device_ids=true, to_apply=%region_14.15 | all-reduce | flops 128 | bytes 1024 | tf_op jit(solution)/shard_map/psum | solution.py:15
  159.4 17.1 %all-reduce.1 = (f32[2,32]{1,0:T(2,128)S(1)}, f32[2,32]{1,0:T(2,128)S(1)}) all-reduce(f32[2,32]{1,0:T(2,128)S(1)} %get-tuple-element.9, f32[2,32]{1,0:T(2,128)S(1)} %get-tuple-element.10), channel_id=1, replica_groups=mesh['img'=16,'patch_0'=4,'patch_1'=4] {'patch_1'}, use_global_device_ids=true, to_apply=%region_15.16 | all-reduce | flops 128 | bytes 1024 | tf_op jit(solution)/shard_map/psum | solution.py:15
  176.6 0.1 mul.129
  176.7 0.1 mul.130
  176.8 0.1 sub.82
  176.9 0.1 sub.83
  177.0 0.2 fusion.67
  177.2 0.0 collective-permute-done
  177.2 0.3 fusion.44
  177.6 0.0 copy-start.6
  177.6 0.0 copy-start.7
  177.6 0.1 slice_dynamic-update-slice_fusion.4
  177.8 0.3 constant_dynamic-update-slice_fusion.1
  178.0 0.1 slice_dynamic-update-slice_fusion.2
  178.2 0.1 slice_dynamic-update-slice_fusion
  178.4 6.4 %fusion.38 = bf16[2,1,128,640]{3,2,1,0:T(8,128)(2,1)} fusion(f32[2,128,640]{2,1,0:T(8,128)S(1)} %get-tuple-element.25, bf16[5760,640,1]{1,0,2:T(8,128)(2,1)} %bitcast.116, bf16[2,1,128,5760]{3,2,0,1:T(8,128)(2,1)S(1)} %slice_dynamic-update-slice_fusion, f32[2,640]{1,0:T(2,128)S(1)} %copy-done.6, f32[640]{0:T(1024)S(1)} %copy-done.7), kind=kOutput, calls=%fused_computation.37 | convolution fusion | flops 1888092160 | bytes 11312640 | tf_op jit(solution)/shard_map/dot_general | solution.py:146
  (24 shorter events, 0.3 us)
Async XLA Ops:
  6.5 141.2 %copy-start = (bf16[640,640]{1,0:T(8,128)(2,1)S(1)}, bf16[640,640]{1,0:T(8,128)(2,1)}, u32[]{:S(2)}) copy-start(bf16[640,640]{1,0:T(8,128)(2,1)} %param.18) | copy-start | bytes 2457604
  6.5 94.4 %all-gather.3.cloned.1.call-start = ((), (), s32[]{:S(2)}) async-start(), calls=%async_computation | async-start | bytes 5570560 | tf_op jit(solution)/shard_map/all_gather | solution.py:100
  10.9 166.3 %collective-permute-start.1 = (bf16[2,1,128,640]{3,2,0,1:T(8,128)(2,1)}, bf16[2,1,128,640]{3,2,0,1:T(8,128)(2,1)S(1)}, u32[]{:S(2)}, u32[]{:S(2)}) collective-permute-start(bf16[2,1,128,640]{3,2,0,1:T(8,128)(2,1)} %bitcast.117), channel_id=1, source_target_pairs={{1,0},{2,1},{3,2},{4,3},{5,4},{6,5},{7,6},{8,7},{9,8},{10,9},{11,1... | collective-permute-start | bytes 983048 | tf_op jit(solution)/shard_map/ppermute | solution.py:26
  12.2 165.0 %collective-permute-start = (bf16[2,1,128,640]{3,2,0,1:T(8,128)(2,1)}, bf16[2,1,128,640]{3,2,0,1:T(8,128)(2,1)S(1)}, u32[]{:S(2)}, u32[]{:S(2)}) collective-permute-start(bf16[2,1,128,640]{3,2,0,1:T(8,128)(2,1)} %bitcast.118), channel_id=1, source_target_pairs={{0,1},{1,2},{2,3},{3,4},{4,5},{5,6},{6,7},{7,8},{8,9},{9,10},{10,1... | collective-permute-start | bytes 983048 | tf_op jit(solution)/shard_map/ppermute | solution.py:23
  129.5 7.0 %copy-start.1 = (f32[2,10,128,2048]{3,2,1,0:T(8,128)}, f32[2,10,128,2048]{3,2,1,0:T(8,128)S(1)}, u32[]{:S(2)}) copy-start(f32[2,10,128,2048]{3,2,1,0:T(8,128)S(1)} %get-tuple-element.24) | copy-start | bytes 62914564
  136.5 10.9 %copy-start.3 = (bf16[2,128,640]{1,2,0:T(8,128)(2,1)S(1)}, bf16[2,128,640]{1,2,0:T(8,128)(2,1)}, u32[]{:S(2)}) copy-start(bf16[2,128,640]{1,2,0:T(8,128)(2,1)} %copy.29) | copy-start | bytes 983044
  147.3 1.0 copy-start.2
  147.4 29.6 %copy-start.4 = (f32[640]{0:T(1024)S(1)}, f32[640]{0:T(1024)}, u32[]{:S(2)}) copy-start(f32[640]{0:T(1024)} %param.20) | copy-start | bytes 7684
  147.4 29.6 %copy-start.5 = (f32[640]{0:T(1024)S(1)}, f32[640]{0:T(1024)}, u32[]{:S(2)}) copy-start(f32[640]{0:T(1024)} %param.19) | copy-start | bytes 7684
  177.6 0.8 copy-start.6
  177.6 0.8 copy-start.7
Sparse Core Ops, SparseCore 0:
  11.0 89.9 all-gather.2
where the time goes:
time: 192 us
  waiting for transfers between devices  75.7 us (39%)
  matrix products  39.7 us (21%)
  blocking collectives  27.3 us (14%)
  local copies, waits for them, and re-layouts  15.5 us (8%)
  between operations  13.7 us (7%)
  other arithmetic  12.5 us (7%)
  starting transfers between devices  7.12 us (4%)
    all_gather x1, waiting for transfers between devices, shards(): block_rows = lax.all_gather(stale_in, PATCH, axis=1, tiled=True)  75.6 us
    psum x2, blocking collectives, over_axes(): return functools.reduce(lax.psum, axes, shard)  27.3 us
    dot_general x1, matrix products, shards(): jnp.einsum('snc,cd->snd', block_rows, w_pair, preferred_element_type=jnp....  13.2 us
    dot_general x2, matrix products, absorb(): jnp.einsum('shqk,skhd->shqd', weights.astype(jnp.bfloat16), values_split,...  11.2 us
    slice x1, local copies, waits for them, and re-layouts, shards(): pair_rows[..., :channels]  10.2 us
    dot_general x1, matrix products, shards(): jnp.dot(unfolded, conv_weight.reshape(9 * channels, channels), preferred_...  6.36 us
    ppermute x1, starting transfers between devices, extended(): lax.ppermute(lax.slice_in_dim(block, block.shape[dim] - width, None, axis...  5.83 us
    dot_general x2, matrix products, absorb(): jnp.einsum('sqhd,skhd->shqk', queries, keys_split, preferred_element_type...  5.51 us
  transfers between devices with their start and end apart: 3, of which 1 were waited for; matrix products, arithmetic and copies ran while one was open for 28% of the time, Pallas kernels for 0%

commit v1 on v0

--- a/solution.py
+++ b/solution.py
@@ -9,6 +9,13 @@
 HEAD_DIM = 64
 PATCH = ("patch_0", "patch_1")
 EPSILON = 1e-05
+
+
+def _list_waves(xx, in_dim):
+    moved = lax.axis_size(PATCH)
+    t_next = jnp.stack([xx] * moved, axis=0)
+    val2 = jnp.concatenate(lax.all_to_all(t_next, PATCH, 0, 0), axis=in_dim)
+    return val2
 
 
 def over_axes(shard, axes):
@@ -97,7 +104,7 @@
         fresh_qkv[..., 2 * channels :],
         no_block,
     )
-    block_rows = lax.all_gather(stale_in, PATCH, axis=1, tiled=True)
+    block_rows = _list_waves(stale_in, 1)
     pair_rows = jnp.einsum(
         "snc,cd->snd", block_rows, w_pair, preferred_element_type=jnp.float32
     ).astype(jnp.bfloat16)

time: 192 us -> 225 us (1.17); the launches traced: 192 us -> 222 us
  waiting for transfers between devices: 75.7 us -> 107 us
  between operations: 13.7 us -> 0.37 us
  starting transfers between devices: 7.12 us -> 18.1 us
  local copies, waits for them, and re-layouts: 15.5 us -> 22 us
  other arithmetic: 12.5 us -> 9.79 us
    all_to_all x0 -> x1, waiting for transfers between devices: none -> 107 us  [_list_waves(): val2 = jnp.concatenate(lax.all_to_all(t_next, PATCH, 0, 0), axis=in_dim)]
    all_gather x1 -> x0, waiting for transfers between devices: 75.6 us -> none  [shards(): block_rows = lax.all_gather(stale_in, PATCH, axis=1, tiled=True)]
    all_to_all x0 -> x1, starting transfers between devices: none -> 11.4 us  [_list_waves(): val2 = jnp.concatenate(lax.all_to_all(t_next, PATCH, 0, 0), axis=in_dim)]
    reshape x0 -> x1, local copies, waits for them, and re-layouts: none -> 3.26 us  [_list_waves(): val2 = jnp.concatenate(lax.all_to_all(t_next, PATCH, 0, 0), axis=in_dim)]
    another operation x0 -> x1, local copies, waits for them, and re-layouts: none -> 3.06 us  [_list_waves(): t_next = jnp.stack([xx] * moved, axis=0)]
  transfers between devices with their start and end apart: 3 -> 3, of which waited for: 1 -> 1; matrix products, arithmetic and copies ran while one was open for 28% -> 24% of each run, Pallas kernels for 0% -> 0%
where the time goes in v1:
time: 225 us; the launch traced here: 222 us
  waiting for transfers between devices  107 us (48%)
  matrix products  38.6 us (17%)
  blocking collectives  25.5 us (11%)
  local copies, waits for them, and re-layouts  22 us (10%)
  starting transfers between devices  18.1 us (8%)
  other arithmetic  9.79 us (4%)
    all_to_all x1, waiting for transfers between devices, _list_waves(): val2 = jnp.concatenate(lax.all_to_all(t_next, PATCH, 0, 0), axis=in_dim)  107 us
    psum x2, blocking collectives, over_axes(): return functools.reduce(lax.psum, axes, shard)  25.5 us
    all_to_all x1, starting transfers between devices, _list_waves(): val2 = jnp.concatenate(lax.all_to_all(t_next, PATCH, 0, 0), axis=in_dim)  11.4 us
    dot_general x1, matrix products, shards(): jnp.einsum('snc,cd->snd', block_rows, w_pair, preferred_element_type=jnp....  11.3 us
    dot_general x2, matrix products, absorb(): jnp.einsum('shqk,skhd->shqd', weights.astype(jnp.bfloat16), values_split,...  11.2 us
    slice x1, local copies, waits for them, and re-layouts, shards(): pair_rows[..., :channels]  10.2 us
    dot_general x2, matrix products, absorb(): jnp.einsum('sqhd,skhd->shqk', queries, keys_split, preferred_element_type...  6.48 us
    dot_general x1, matrix products, shards(): jnp.dot(unfolded, conv_weight.reshape(9 * channels, channels), preferred_...  6.36 us
  transfers between devices with their start and end apart: 3, of which 1 were waited for; matrix products, arithmetic and copies ran while one was open for 24% of the time, Pallas kernels for 0%

profile of v1, /device:TPU:2, one launch (start us, length us, event | category | flops | bytes accessed | tf_op | source)
XLA Modules:
  0.0 221.6 jit_solution(6152872311339758886)
XLA Ops:
  0.0 1.2 convert_reduce_fusion.1
  1.2 1.2 fusion.53
  2.4 1.2 fusion.59
  3.6 3.1 %stack.3 = bf16[16,2,128,640]{3,2,1,0:T(8,128)(2,1)} broadcast(bf16[2,128,640]{2,1,0:T(8,128)(2,1)S(1)} %fusion.59), dimensions={1,2,3} | broadcast | bytes 5570560 | tf_op jit(solution)/shard_map/stack | solution.py:16
  6.7 11.4 %all-to-all-start = ((bf16[16,2,128,640]{3,2,1,0:T(8,128)(2,1)}), bf16[16,2,128,640]{3,2,1,0:T(8,128)(2,1)}, u32[]{:S(2)}, u32[]{:S(2)}) async-start(bf16[16,2,128,640]{3,2,1,0:T(8,128)(2,1)} %stack.3), calls=%async_computation | async-start | bytes 10485760 | tf_op jit(solution)/shard_map/all_to_all | solution.py:17
  18.1 1.3 collective-permute-start.1
  19.4 5.5 %collective-permute-start = (bf16[2,1,128,640]{3,2,0,1:T(8,128)(2,1)}, bf16[2,1,128,640]{3,2,0,1:T(8,128)(2,1)S(1)}, u32[]{:S(2)}, u32[]{:S(2)}) collective-permute-start(bf16[2,1,128,640]{3,2,0,1:T(8,128)(2,1)} %bitcast), channel_id=1, source_target_pairs={{0,1},{1,2},{2,3},{3,4},{4,5},{5,6},{6,7},{7,8},{8,9},{9,10},{10,1... | collective-permute-start | bytes 983048 | tf_op jit(solution)/shard_map/ppermute | solution.py:30
  24.9 0.1 convert_reduce_fusion
  25.0 0.2 fusion.49
  25.2 2.8 %convolution_convert_fusion.1 = bf16[2,128,1920]{2,1,0:T(8,128)(2,1)S(1)} fusion(bf16[640,1920]{1,0:T(8,128)(2,1)} %param.17, bf16[2,1,128,640]{3,2,1,0:T(8,128)(2,1)S(1)} %copy-done.2, f32[640]{0:T(1024)S(1)} %copy-done.6, f32[640]{0:T(1024)S(1)} %copy-done.7, f32[2,128]{1,0:T(2,128)S(1)} %add_rsqrt_fusion.2, f32[2,128]{1,0:T(2,128)S(1)} %broadcast_multiply_fusion.2), kind=kOutput, calls=%fused_computation.12 | convolution fusion | flops 630620160 | bytes 3775488 | tf_op jit(solution)/shard_map/stc,cd->std/dot_general | solution.py:89
  28.0 0.1 fusion.78
  28.1 0.2 copy.38
  28.3 0.9 copy.39
  29.2 0.9 copy.40
  30.1 1.4 fusion.79
  31.5 0.2 fusion.40
  31.7 107.1 %all-to-all-done = bf16[16,2,128,640]{3,2,1,0:T(8,128)(2,1)} async-done(((bf16[16,2,128,640]{3,2,1,0:T(8,128)(2,1)}), bf16[16,2,128,640]{3,2,1,0:T(8,128)(2,1)}, u32[]{:S(2)}, u32[]{:S(2)}) %all-to-all-start) | async-done | bytes 5242912 | tf_op jit(solution)/shard_map/all_to_all | solution.py:17
  138.9 3.3 %copy.43 = bf16[2,16,128,640]{3,2,1,0:T(8,128)(2,1)S(1)} copy(bf16[2,16,128,640]{3,2,0,1:T(8,128)(2,1)} %bitcast.12) | data formatting | bytes 10485760 | tf_op jit(solution)/shard_map/reshape | solution.py:17
  142.2 11.3 %convolution_convert_fusion = bf16[2,2048,1280]{1,2,0:T(8,128)(2,1)} fusion(bf16[2,2048,640]{2,1,0:T(8,128)(2,1)S(1)} %bitcast.113, bf16[640,1920]{1,0:T(8,128)(2,1)S(1)} %copy-done.8), kind=kOutput, calls=%fused_computation.5 | convolution fusion | flops 6716129280 | bytes 17367040 | tf_op jit(solution)/shard_map/snc,cd->snd/dot_general | solution.py:108
  153.4 10.2 %fusion.77 = (bf16[2,2048,640]{1,2,0:T(8,128)(2,1)}, bf16[2,2048,640]{1,2,0:T(8,128)(2,1)}) fusion(bf16[2,2048,1280]{1,2,0:T(8,128)(2,1)} %convolution_convert_fusion), kind=kLoop, calls=%fused_computation.99 | loop fusion | bytes 20971520 | tf_op jit(solution)/shard_map/slice | solution.py:114
  163.6 5.1 %fusion = (f32[2,10,128]{2,1,0:T(8,128)S(1)}, f32[2,10,128,2048]{3,2,1,0:T(8,128)S(1)}) fusion(pred[2048]{0:T(1024)(128)(4,1)S(1)} %fusion.72, bf16[2,128,10,64]{1,3,2,0:T(8,128)(2,1)S(1)} %bitcast.115, bf16[2,2048,10,64]{1,3,2,0:T(8,128)(2,1)} %bitcast.111), kind=kOutput, calls=%fused_computation.2 | convolution fusion | flops 686814720 | bytes 26554368 | tf_op jit(solution)/shard_map/sqhd,skhd->shqk/dot_general | solution.py:52
  168.7 4.7 %fusion.1 = f32[2,10,128]{2,1,0:T(8,128)S(1)} fusion(f32[2,10,128,2048]{3,2,1,0:T(8,128)S(1)} %get-tuple-element.24, f32[2,10,128]{2,1,0:T(8,128)S(1)} %max.18, pred[2048]{0:T(1024)(128)(4,1)S(1)} %fusion.72), kind=kLoop, calls=%fused_computation.3 | loop fusion | flops 20968960 | bytes 20994048 | tf_op jit(solution)/shard_map/reduce_sum | solution.py:59
  173.4 2.3 %copy-done.1 = f32[2,10,128,2048]{3,2,1,0:T(8,128)} copy-done((f32[2,10,128,2048]{3,2,1,0:T(8,128)}, f32[2,10,128,2048]{3,2,1,0:T(8,128)S(1)}, u32[]{:S(2)}) %copy-start.1) | copy-done | bytes 20971544
  175.7 10.8 %fusion.16 = f32[2,128,10,64]{1,3,2,0:T(8,128)S(1)} fusion(bf16[2,2048,10,64]{1,3,2,0:T(8,128)(2,1)} %bitcast.112, f32[2,10,128,2048]{3,2,1,0:T(8,128)} %copy-done.1, f32[2,10,128]{2,1,0:T(8,128)S(1)} %max.18, pred[2048]{0:T(1024)(128)(4,1)S(1)} %fusion.72), kind=kOutput, calls=%fused_computation.25 | convolution fusion | flops 692060160 | bytes 26882048 | tf_op jit(solution)/shard_map/shqk,skhd->shqd/dot_general | solution.py:60
  186.6 0.0 copy-start.4
  186.6 0.0 copy-start.5
  186.6 0.3 fusion.30
  187.0 0.5 fusion.75
  187.5 0.1 reduce_sum.102
  187.6 0.1 reduce_sum.99
  187.7 0.1 reduce_sum.103
  187.8 0.1 reduce_sum.100
  187.9 16.7 %all-reduce.2 = (f32[2,32]{1,0:T(2,128)S(1)}, f32[2,32]{1,0:T(2,128)S(1)}) all-reduce(f32[2,32]{1,0:T(2,128)S(1)} %reduce_sum.103, f32[2,32]{1,0:T(2,128)S(1)} %reduce_sum.100), channel_id=1, replica_groups=mesh['img'=16,'patch_0'=4,'patch_1'=4] {'patch_0'}, use_global_device_ids=true, to_apply=%region_14.15 | all-reduce | flops 128 | bytes 1024 | tf_op jit(solution)/shard_map/psum | solution.py:22
  204.6 8.8 %all-reduce.1 = (f32[2,32]{1,0:T(2,128)S(1)}, f32[2,32]{1,0:T(2,128)S(1)}) all-reduce(f32[2,32]{1,0:T(2,128)S(1)} %get-tuple-element.9, f32[2,32]{1,0:T(2,128)S(1)} %get-tuple-element.10), channel_id=1, replica_groups=mesh['img'=16,'patch_0'=4,'patch_1'=4] {'patch_1'}, use_global_device_ids=true, to_apply=%region_15.16 | all-reduce | flops 128 | bytes 1024 | tf_op jit(solution)/shard_map/psum | solution.py:22
  213.4 0.1 mul.129
  213.5 0.1 mul.130
  213.6 0.1 sub.82
  213.7 0.1 sub.83
  213.8 0.2 fusion.67
  214.1 0.0 collective-permute-done.1
  214.1 0.3 fusion.43
  214.4 0.0 copy-start.9
  214.4 0.0 copy-start.10
  214.5 0.1 slice_dynamic-update-slice_fusion.4
  214.6 0.3 constant_dynamic-update-slice_fusion.1
  214.9 0.1 slice_dynamic-update-slice_fusion.2
  215.1 0.1 slice_dynamic-update-slice_fusion
  215.2 6.4 %fusion.37 = bf16[2,1,128,640]{3,2,1,0:T(8,128)(2,1)} fusion(f32[2,128,640]{2,1,0:T(8,128)S(1)} %get-tuple-element.25, bf16[5760,640,1]{1,0,2:T(8,128)(2,1)} %bitcast.119, bf16[2,1,128,5760]{3,2,0,1:T(8,128)(2,1)S(1)} %slice_dynamic-update-slice_fusion, f32[2,640]{1,0:T(2,128)S(1)} %copy-done.9, f32[640]{0:T(1024)S(1)} %copy-done.10), kind=kOutput, calls=%fused_computation.36 | convolution fusion | flops 1888092160 | bytes 11312640 | tf_op jit(solution)/shard_map/dot_general | solution.py:153
  (31 shorter events, 0.3 us)
Async XLA Ops:
  0.0 187.0 %copy-start = (bf16[640,640]{1,0:T(8,128)(2,1)S(1)}, bf16[640,640]{1,0:T(8,128)(2,1)}, u32[]{:S(2)}) copy-start(bf16[640,640]{1,0:T(8,128)(2,1)} %param.18) | copy-start | bytes 2457604
  6.7 18.2 %copy-start.2 = (bf16[2,1,128,640]{3,2,1,0:T(8,128)(2,1)S(1)}, bf16[2,1,128,640]{3,2,1,0:T(8,128)(2,1)}, u32[]{:S(2)}) copy-start(bf16[2,1,128,640]{3,2,1,0:T(8,128)(2,1)} %param.12) | copy-start | bytes 983044
  6.7 18.6 %copy-start.6 = (f32[640]{0:T(1024)S(1)}, f32[640]{0:T(1024)}, u32[]{:S(2)}) copy-start(f32[640]{0:T(1024)} %param.16) | copy-start | bytes 7684
  6.7 18.6 %copy-start.7 = (f32[640]{0:T(1024)S(1)}, f32[640]{0:T(1024)}, u32[]{:S(2)}) copy-start(f32[640]{0:T(1024)} %param.15) | copy-start | bytes 7684
  6.7 132.2 %all-to-all-start = ((bf16[16,2,128,640]{3,2,1,0:T(8,128)(2,1)}), bf16[16,2,128,640]{3,2,1,0:T(8,128)(2,1)}, u32[]{:S(2)}, u32[]{:S(2)}) async-start(bf16[16,2,128,640]{3,2,1,0:T(8,128)(2,1)} %stack.3), calls=%async_computation | async-start | bytes 10485760 | tf_op jit(solution)/shard_map/all_to_all | solution.py:17
  18.1 196.0 %collective-permute-start.1 = (bf16[2,1,128,640]{3,2,0,1:T(8,128)(2,1)}, bf16[2,1,128,640]{3,2,0,1:T(8,128)(2,1)S(1)}, u32[]{:S(2)}, u32[]{:S(2)}) collective-permute-start(bf16[2,1,128,640]{3,2,0,1:T(8,128)(2,1)} %bitcast), channel_id=1, source_target_pairs={{1,0},{2,1},{3,2},{4,3},{5,4},{6,5},{7,6},{8,7},{9,8},{10,9},{11,1... | collective-permute-start | bytes 983048 | tf_op jit(solution)/shard_map/ppermute | solution.py:33
  19.4 194.7 %collective-permute-start = (bf16[2,1,128,640]{3,2,0,1:T(8,128)(2,1)}, bf16[2,1,128,640]{3,2,0,1:T(8,128)(2,1)S(1)}, u32[]{:S(2)}, u32[]{:S(2)}) collective-permute-start(bf16[2,1,128,640]{3,2,0,1:T(8,128)(2,1)} %bitcast), channel_id=1, source_target_pairs={{0,1},{1,2},{2,3},{3,4},{4,5},{5,6},{6,7},{7,8},{8,9},{9,10},{10,1... | collective-permute-start | bytes 983048 | tf_op jit(solution)/shard_map/ppermute | solution.py:30
  138.9 3.3 %copy-start.8 = (bf16[640,1920]{1,0:T(8,128)(2,1)S(1)}, bf16[640,1920]{1,0:T(8,128)(2,1)}, u32[]{:S(2)}) copy-start(bf16[640,1920]{1,0:T(8,128)(2,1)} %param.17) | copy-start | bytes 7372804
  168.7 7.0 %copy-start.1 = (f32[2,10,128,2048]{3,2,1,0:T(8,128)}, f32[2,10,128,2048]{3,2,1,0:T(8,128)S(1)}, u32[]{:S(2)}) copy-start(f32[2,10,128,2048]{3,2,1,0:T(8,128)S(1)} %get-tuple-element.24) | copy-start | bytes 62914564
  175.7 10.9 %copy-start.3 = (bf16[2,128,640]{1,2,0:T(8,128)(2,1)S(1)}, bf16[2,128,640]{1,2,0:T(8,128)(2,1)}, u32[]{:S(2)}) copy-start(bf16[2,128,640]{1,2,0:T(8,128)(2,1)} %copy.40) | copy-start | bytes 983044
  186.6 27.2 %copy-start.4 = (f32[640]{0:T(1024)S(1)}, f32[640]{0:T(1024)}, u32[]{:S(2)}) copy-start(f32[640]{0:T(1024)} %param.20) | copy-start | bytes 7684
  186.6 27.2 %copy-start.5 = (f32[640]{0:T(1024)S(1)}, f32[640]{0:T(1024)}, u32[]{:S(2)}) copy-start(f32[640]{0:T(1024)} %param.19) | copy-start | bytes 7684
  214.4 0.8 copy-start.9
  214.4 0.8 copy-start.10
